TPU v7x, 32 devices: a whole 2x2x4 slice. The times are simulated.
32 devices in a mesh: groups: 2 (over x), tm: 8 (over z, y), sector: 2 (over core).
Axes of the slice: x: 2, y: 2, z: 4, core: 2. Of those that a mesh axis runs over, the one named last changes fastest.
Arguments:
- context: bfloat16 [16, 2, 512, 256], P(('groups', 'tm'), 'sector'), parts along dimension 0, may hold values from -6 to 6
- depth_weight: float32 [16, 2, 16, 512], P(('groups', 'tm'), 'sector'), parts along dimension 0, may hold values from 0 to 1
- cell_ids: int32 [2, 16, 512], P('sector'), may hold values from 0 to 4095
- time_embed: bfloat16 [8, 256], replicated, may hold values from -3 to 3
- norm_gain: float32 [2, 2, 256], replicated, may hold values from 0.1 to 1.9
- w_qkv: bfloat16 [2, 256, 768], replicated, may hold values from -15 to 15
- w_out: bfloat16 [2, 256, 256], replicated, may hold values from -0.375 to 0.375
- w_up: bfloat16 [2, 256, 1024], replicated, may hold values from -0.375 to 0.375
- w_down: bfloat16 [2, 1024, 256], replicated, may hold values from -0.1875 to 0.1875
- conv_weight: bfloat16 [3, 3, 256, 256], replicated, may hold values from -0.125 to 0.125
Outputs:
- bev_out: bfloat16 [16, 64, 64, 256], P(('groups', 'tm'), 'sector'), parts along dimension 0
There are 2 independent parts, one for each index of `groups`. A program takes and returns all parts, laid end to end along the dimension named above; an argument that names none is the same for every part. Nothing has to cross between parts.
All inputs are finite; a program needn't handle non-finite values.
Results may differ from a plain program's by a relative error of at most 0.0079.
Values may be sent and summed in bfloat16 or wider, within the bound.
No kernel may reach another device: no remote copies, remote signals or barrier semaphores. Data moves between devices by JAX's collectives and lax.ppermute only.
A program may use at most 128 MiB of HBM per device.

v0:
```python
import jax
import jax.numpy as jnp
from jax import lax
from jax.sharding import PartitionSpec as P

HEADS = 8
GRID = 64


def padded_2(cells, sides, width):
    for axis, dim in sides:
        count = lax.axis_size(axis)
        ends = count - 1
        head = lax.slice_in_dim(cells, 0, width, axis=dim)
        tail = lax.slice_in_dim(cells, cells.shape[dim] - width, cells.shape[dim], axis=dim)
        cells = jnp.concatenate(
            [
                lax.ppermute(tail, axis, [(i, (i + 1) % count) for i in range(ends)]),
                cells,
                lax.ppermute(head, axis, [((i + 1) % count, i) for i in range(ends)]),
            ],
            axis=dim,
        )
    return cells


def pool_local(context, depth_weight, cell_ids):
    cell_count = GRID * GRID
    block_cells = min(512, cell_count)
    cell_index = cell_ids[0]

    def one_frame(frame_inputs):
        features, weights = frame_inputs

        def one_block(first_cell):
            target = first_cell + lax.broadcasted_iota(jnp.int32, (block_cells, 1), 0)
            matches = cell_index[:, None, :] == target[None]
            matrix = jnp.sum(
                jnp.where(matches, weights[:, None, :], jnp.zeros_like(weights[:, None, :])), axis=0
            ).astype(jnp.bfloat16)
            return jnp.dot(matrix, features, preferred_element_type=jnp.float32).astype(
                jnp.bfloat16
            )

        starts = jnp.arange(cell_count // block_cells) * block_cells
        return lax.map(one_block, starts).reshape(cell_count, features.shape[-1])

    return lax.map(one_frame, (context[:, 0], depth_weight[:, 0]))


def normalize(values, gain):
    return values * lax.rsqrt(jnp.mean(values * values, axis=-1, keepdims=True) + 1e-05) * gain


def encode_stack(tokens, time_embed, norm_gain, w_qkv, w_out, w_up, w_down):
    frame_count, cell_count, channels = tokens.shape
    head_size = channels // HEADS
    query_frame = lax.broadcasted_iota(jnp.int32, (frame_count, frame_count), 0)
    key_frame = lax.broadcasted_iota(jnp.int32, (frame_count, frame_count), 1)
    allowed = key_frame <= query_frame
    stream = (tokens.astype(jnp.float32) + time_embed[:, None, :].astype(jnp.float32)).reshape(
        frame_count * cell_count, channels
    )
    for number in range(w_qkv.shape[0]):
        normed = normalize(stream, norm_gain[number, 0]).astype(jnp.bfloat16)
        projected = jnp.dot(normed, w_qkv[number], preferred_element_type=jnp.float32).astype(
            jnp.bfloat16
        )
        projected = projected.reshape(frame_count, cell_count, 3, HEADS, head_size)
        scores = jnp.einsum(
            "fchd,gchd->chfg",
            projected[:, :, 0],
            projected[:, :, 1],
            preferred_element_type=jnp.float32,
        ) * head_size ** (-0.5)
        scores = jnp.where(allowed, scores, -1e30)
        largest = jnp.max(scores, axis=-1, keepdims=True)
        raised = jnp.exp(scores - largest)
        soft_weights = (raised / jnp.sum(raised, axis=-1, keepdims=True)).astype(jnp.bfloat16)
        mixed = jnp.einsum(
            "chfg,gchd->fchd", soft_weights, projected[:, :, 2], preferred_element_type=jnp.float32
        ).astype(jnp.bfloat16)
        mixed = mixed.reshape(frame_count * cell_count, channels)
        stream = stream + jnp.dot(mixed, w_out[number], preferred_element_type=jnp.float32)
        normed_second = normalize(stream, norm_gain[number, 1]).astype(jnp.bfloat16)
        hidden_units = jax.nn.gelu(
            jnp.dot(normed_second, w_up[number], preferred_element_type=jnp.float32),
            approximate=True,
        ).astype(jnp.bfloat16)
        stream = stream + jnp.dot(hidden_units, w_down[number], preferred_element_type=jnp.float32)
    return stream.reshape(frame_count, cell_count, channels).astype(jnp.bfloat16)


def encode_return(tokens, weights):
    encoded = encode_stack(tokens, *weights)
    return lax.all_to_all(encoded, "tm", split_axis=0, concat_axis=1, tiled=True)


def body(
    context, depth_weight, cell_ids, time_embed, norm_gain, w_qkv, w_out, w_up, w_down, conv_weight
):
    partial_value = lax.optimization_barrier(pool_local(context, depth_weight, cell_ids))
    frames_dev, cell_count, channels = partial_value.shape
    tm_count = lax.axis_size("tm")
    band_cells = cell_count // lax.axis_size("sector")
    piece_cells = band_cells // tm_count
    weights = (time_embed, norm_gain, w_qkv, w_out, w_up, w_down)
    pooled = (
        lax.psum_scatter(partial_value, "sector", scatter_dimension=1, tiled=True)
        .astype(jnp.float32)
        .astype(jnp.bfloat16)
    )
    sectioned = pooled.reshape(frames_dev, tm_count, piece_cells, channels)
    received = lax.all_to_all(sectioned, "tm", split_axis=1, concat_axis=0, tiled=True)
    tokens = received.reshape(received.shape[0], received.shape[2], channels)
    returned = encode_return(tokens, weights)
    item_count = returned.shape[1] // tm_count
    result = returned.reshape(frames_dev, tm_count, item_count, channels)
    row_count = band_cells // GRID
    encoded = result.reshape(frames_dev, row_count, GRID, channels)
    padded = padded_2(encoded, (("sector", 1),), 1)
    padded = jnp.pad(padded, ((0, 0), (0, 0), (1, 1), (0, 0)))
    summed = encoded.astype(jnp.float32)
    for offset in range(3):
        row_strip = padded[:, offset : offset + row_count]
        stacked = jnp.concatenate(
            [row_strip[:, :, column : column + GRID] for column in range(3)], axis=-1
        )
        product = jnp.dot(
            stacked.reshape(frames_dev * row_count * GRID, 3 * channels),
            conv_weight[offset].reshape(3 * channels, channels),
            preferred_element_type=jnp.float32,
        )
        summed = summed + product.reshape(summed.shape)
    return summed.astype(jnp.bfloat16)


def solution(mesh):
    return jax.shard_map(
        body,
        mesh=mesh,
        in_specs=(
            P(("groups", "tm"), "sector", None, None),
            P(("groups", "tm"), "sector", None, None),
            P("sector", None, None),
            P(),
            P(),
            P(),
            P(),
            P(),
            P(),
            P(),
        ),
        out_specs=P(("groups", "tm"), "sector", None, None),
        check_vma=False,
    )
```

profile of v0, /device:TPU:0, one launch (start us, length us, event | category | flops | bytes accessed | tf_op | source)
XLA Modules:
  0.0 295.6 jit_solution(16586934135951967975)
XLA Ops:
  6.5 45.5 %while.17 = (s32[]{:T(128)}, bf16[8,512,256]{2,1,0:T(8,128)(2,1)}, s32[1,16,512]{2,1,0:T(8,128)}, s32[8]{0:T(128)S(1)}, f32[16,512]{1,0:T(8,128)}, /*index=5*/bf16[512,256]{1,0:T(8,128)(2,1)}, s32[]{:T(128)}) while((s32[]{:T(128)}, bf16[8,512,256]{2,1,0:T(8,128)(2,1)}, s32[1,16,512]{2,1,0:T(8,128)}, s32[8]{0:T(128)S(1)}, f32[16,512]{1,0:T(8,128)}, ...), condition=%wide.region_2.3_spmd, body=%wide.region_0.2_spmd.sunk | while | flops 146670080 | bytes 1643101 | solution.py:46
  52.0 12.6 %reduce-scatter.2.cloned.1.call-done = bf16[1,2048,256]{2,1,0:T(8,128)(2,1)} async-done(((bf16[1,4096,256]{2,1,0:T(8,128)(2,1)}), bf16[1,2048,256]{2,1,0:T(8,128)(2,1)}) %reduce-scatter.2.cloned.1.call-update) | async-done | bytes 1048592 | tf_op jit(solution)/shard_map/reduce_scatter | solution.py:109
  64.7 6.2 %all-to-all-start = ((bf16[1,8,256,256]{3,2,0,1:T(8,128)(2,1)}), bf16[1,8,256,256]{3,2,0,1:T(8,128)(2,1)S(1)}, u32[]{:S(2)}, u32[]{:S(2)}) async-start(bf16[1,8,256,256]{3,2,0,1:T(8,128)(2,1)} %bitcast.169), calls=%async_computation.1 | async-start | bytes 2097152 | tf_op jit(solution)/shard_map/all_to_all | solution.py:114
  70.9 26.0 %all-to-all-done = bf16[1,8,256,256]{3,2,0,1:T(8,128)(2,1)S(1)} async-done(((bf16[1,8,256,256]{3,2,0,1:T(8,128)(2,1)}), bf16[1,8,256,256]{3,2,0,1:T(8,128)(2,1)S(1)}, u32[]{:S(2)}, u32[]{:S(2)}) %all-to-all-start) | async-done | bytes 1048608 | tf_op jit(solution)/shard_map/all_to_all | solution.py:114
  106.1 7.2 %copy.70 = bf16[8,256,1,8,32]{4,0,3,1,2:T(8,128)(2,1)} copy(bf16[8,256,1,8,32]{1,0,4,3,2:T(8,128)(2,1)S(1)} %get-tuple-element.69) | data formatting | bytes 2097152
  113.2 7.2 %copy.71 = bf16[8,256,1,8,32]{4,0,3,1,2:T(8,128)(2,1)} copy(bf16[8,256,1,8,32]{1,0,4,3,2:T(8,128)(2,1)S(1)} %get-tuple-element.70) | data formatting | bytes 2097152
  120.4 9.0 %fusion.26 = f32[256,8,8,8]{2,3,1,0:T(8,128)} fusion(bf16[8,256,1,8,32]{4,0,3,1,2:T(8,128)(2,1)} %copy.71, bf16[8,256,1,8,32]{4,0,3,1,2:T(8,128)(2,1)} %copy.70), kind=kOutput, calls=%fused_computation.31 | convolution fusion | flops 8388608 | bytes 2621440 | tf_op jit(solution)/shard_map/fchd,gchd->chfg/dot_general | solution.py:70
  129.4 6.4 %copy.59 = f32[256,8,8,8]{0,3,2,1:T(8,128)S(1)} copy(f32[256,8,8,8]{2,3,1,0:T(8,128)} %fusion.26) | data formatting | bytes 1048576 | tf_op jit(solution)/shard_map/fchd,gchd->chfg/dot_general | solution.py:70
  136.9 6.4 %copy.60 = bf16[256,8,8,8]{3,2,1,0:T(8,128)(2,1)} copy(bf16[256,8,8,8]{0,3,2,1:T(8,128)(2,1)S(1)} %divide_convert_fusion.1) | data formatting | bytes 524288 | tf_op jit(solution)/shard_map/convert_element_type | solution.py:79
  143.3 7.7 %copy.69 = bf16[8,256,1,8,32]{4,0,3,1,2:T(8,128)(2,1)} copy(bf16[8,256,1,8,32]{1,0,4,3,2:T(8,128)(2,1)S(1)} %get-tuple-element.68) | data formatting | bytes 2097152
  151.0 7.8 %convert_bitcast_fusion.1 = bf16[8,256,8,32]{3,0,2,1:T(8,128)(2,1)} fusion(bf16[256,8,8,8]{3,2,1,0:T(8,128)(2,1)} %copy.60, bf16[8,256,1,8,32]{4,0,3,1,2:T(8,128)(2,1)} %copy.69), kind=kOutput, calls=%fused_computation.37 | convolution fusion | flops 8912896 | bytes 2359296 | tf_op jit(solution)/shard_map/chfg,gchd->fchd/dot_general | solution.py:80
  158.8 6.0 %copy.61 = bf16[8,256,8,32]{1,0,3,2:T(8,128)(2,1)S(1)} copy(bf16[8,256,8,32]{3,0,2,1:T(8,128)(2,1)} %convert_bitcast_fusion.1) | data formatting | bytes 2097152 | tf_op jit(solution)/shard_map/convert_element_type | solution.py:82
  166.4 5.9 %multiply_reduce_fusion.1 = (f32[2048]{0:T(1024)S(1)}, f32[2048,256]{1,0:T(8,128)}) fusion(f32[2048,256]{1,0:T(8,128)S(1)} %get-tuple-element.89, bf16[2,1024,256]{2,1,0:T(8,128)(2,1)} %param.20, f32[256]{0:T(256)S(1)} %bitcast.179, f32[2048]{0:T(1024)S(1)} %add_rsqrt_fusion.2, bf16[2,256,1024]{2,1,0:T(8,128)(2,1)} %param.19), kind=kOutput, calls=%fused_computation.83 | convolution fusion | flops 2169501696 | bytes 7357440 | tf_op jit(solution)/shard_map/dot_general | solution.py:90
  175.0 3.1 %copy.62 = bf16[2048,768]{0,1:T(8,128)(2,1)} copy(bf16[2048,768]{1,0:T(8,128)(2,1)S(1)} %convolution_convert_fusion.1) | data formatting | bytes 6291456 | tf_op jit(solution)/shard_map/convert_element_type | solution.py:66
  181.4 7.2 %copy.73 = bf16[8,256,1,8,32]{4,0,3,1,2:T(8,128)(2,1)} copy(bf16[8,256,1,8,32]{1,0,4,3,2:T(8,128)(2,1)S(1)} %get-tuple-element.66) | data formatting | bytes 2097152
  188.5 7.2 %copy.74 = bf16[8,256,1,8,32]{4,0,3,1,2:T(8,128)(2,1)} copy(bf16[8,256,1,8,32]{1,0,4,3,2:T(8,128)(2,1)S(1)} %get-tuple-element.67) | data formatting | bytes 2097152
  195.7 9.0 %fusion.21 = f32[256,8,8,8]{2,3,1,0:T(8,128)} fusion(bf16[8,256,1,8,32]{4,0,3,1,2:T(8,128)(2,1)} %copy.74, bf16[8,256,1,8,32]{4,0,3,1,2:T(8,128)(2,1)} %copy.73), kind=kOutput, calls=%fused_computation.26 | convolution fusion | flops 8388608 | bytes 2621440 | tf_op jit(solution)/shard_map/fchd,gchd->chfg/dot_general | solution.py:70
  204.7 6.4 %copy.66 = f32[256,8,8,8]{0,3,2,1:T(8,128)S(1)} copy(f32[256,8,8,8]{2,3,1,0:T(8,128)} %fusion.21) | data formatting | bytes 1048576 | tf_op jit(solution)/shard_map/fchd,gchd->chfg/dot_general | solution.py:70
  212.2 6.4 %copy.67 = bf16[256,8,8,8]{3,2,1,0:T(8,128)(2,1)} copy(bf16[256,8,8,8]{0,3,2,1:T(8,128)(2,1)S(1)} %divide_convert_fusion) | data formatting | bytes 524288 | tf_op jit(solution)/shard_map/convert_element_type | solution.py:79
  218.6 7.4 %copy.72 = bf16[8,256,1,8,32]{4,0,3,1,2:T(8,128)(2,1)} copy(bf16[8,256,1,8,32]{1,0,4,3,2:T(8,128)(2,1)S(1)} %get-tuple-element.65) | data formatting | bytes 2097152
  226.0 7.8 %convert_bitcast_fusion = bf16[8,256,8,32]{3,0,2,1:T(8,128)(2,1)} fusion(bf16[256,8,8,8]{3,2,1,0:T(8,128)(2,1)} %copy.67, bf16[8,256,1,8,32]{4,0,3,1,2:T(8,128)(2,1)} %copy.72), kind=kOutput, calls=%fused_computation.36 | convolution fusion | flops 8912896 | bytes 2359296 | tf_op jit(solution)/shard_map/chfg,gchd->fchd/dot_general | solution.py:80
  233.7 6.0 %copy.68 = bf16[8,256,8,32]{1,0,3,2:T(8,128)(2,1)S(1)} copy(bf16[8,256,8,32]{3,0,2,1:T(8,128)(2,1)} %convert_bitcast_fusion) | data formatting | bytes 2097152 | tf_op jit(solution)/shard_map/convert_element_type | solution.py:82
  242.0 5.6 %fusion.70 = bf16[2048,256]{1,0:T(8,128)(2,1)S(1)} fusion(f32[2048,256]{1,0:T(8,128)} %get-tuple-element.95, f32[256]{0:T(256)S(1)} %bitcast.178, f32[2048]{0:T(1024)S(1)} %add_rsqrt_fusion, bf16[2,1024,256]{2,1,0:T(8,128)(2,1)} %param.20, bf16[2,256,1024]{2,1,0:T(8,128)(2,1)} %param.19), kind=kOutput, calls=%fused_computation.72 | convolution fusion | flops 2168979456 | bytes 6300672 | tf_op jit(solution)/shard_map/dot_general | solution.py:90
  247.6 29.3 %all_to_all.8 = bf16[8,256,256]{2,1,0:T(8,128)(2,1)S(1)} all-to-all(bf16[8,256,256]{2,1,0:T(8,128)(2,1)S(1)} %bitcast.170), channel_id=1, replica_groups=mesh['groups'=2,'tm'=8,'sector'=2] {'tm'}, dimensions={0} | all-to-all | bytes 2097152 | tf_op jit(solution)/shard_map/all_to_all | solution.py:96
  (86 shorter events, 77.8 us)
Async XLA Ops:
  6.5 58.1 %reduce-scatter.2.cloned.1.call-start = ((), (), s32[]{:S(2)}) async-start(), calls=%async_computation.3 | async-start | bytes 3145728 | tf_op jit(solution)/shard_map/reduce_scatter | solution.py:109
  52.0 18.9 %copy-start.5 = (bf16[8,256]{1,0:T(8,128)(2,1)S(1)}, bf16[8,256]{1,0:T(8,128)(2,1)}, u32[]{:S(2)}) copy-start(bf16[8,256]{1,0:T(8,128)(2,1)} %param.15) | copy-start | bytes 12292
  52.0 18.9 %copy-start.6 = (f32[2,2,256]{2,1,0:T(2,128)S(1)}, f32[2,2,256]{2,1,0:T(2,128)}, u32[]{:S(2)}) copy-start(f32[2,2,256]{2,1,0:T(2,128)} %param.16) | copy-start | bytes 12292
  64.7 32.3 %all-to-all-start = ((bf16[1,8,256,256]{3,2,0,1:T(8,128)(2,1)}), bf16[1,8,256,256]{3,2,0,1:T(8,128)(2,1)S(1)}, u32[]{:S(2)}, u32[]{:S(2)}) async-start(bf16[1,8,256,256]{3,2,0,1:T(8,128)(2,1)} %bitcast.169), calls=%async_computation.1 | async-start | bytes 2097152 | tf_op jit(solution)/shard_map/all_to_all | solution.py:114
  96.9 1.0 copy-start
  158.7 6.3 %copy-start.1 = (bf16[1,8,256,256]{3,2,0,1:T(8,128)(2,1)S(1)}, bf16[1,8,256,256]{3,2,0,1:T(8,128)(2,1)}, u32[]{:S(2)}) copy-start(bf16[1,8,256,256]{3,2,0,1:T(8,128)(2,1)} %copy-done) | copy-start | bytes 3145732
  164.7 1.0 copy-start.4
  233.7 6.3 %copy-start.2 = (f32[2048,256]{1,0:T(8,128)S(1)}, f32[2048,256]{1,0:T(8,128)}, u32[]{:S(2)}) copy-start(f32[2048,256]{1,0:T(8,128)} %get-tuple-element.91) | copy-start | bytes 6291460
  242.0 37.6 %copy-start.3 = (bf16[3,3,256,256]{3,2,1,0:T(8,128)(2,1)S(1)}, bf16[3,3,256,256]{3,2,1,0:T(8,128)(2,1)}, u32[]{:S(2)}) copy-start(bf16[3,3,256,256]{3,2,1,0:T(8,128)(2,1)} %param.21) | copy-start | bytes 3538948
  277.0 2.7 collective-permute-start
  278.3 3.1 %collective-permute-start.1 = (bf16[1,1,64,256]{3,2,1,0:T(8,128)(2,1)S(1)}, bf16[1,1,64,256]{3,2,1,0:T(8,128)(2,1)S(1)}, u32[]{:S(2)}, u32[]{:S(2)}) collective-permute-start(bf16[1,1,64,256]{3,2,1,0:T(8,128)(2,1)S(1)} %get-tuple-element.81), channel_id=1, source_target_pairs={{1,0},{3,2},{5,4},{7,6},{9,8},{11,10},{13,12},{15,14},{17,16},{19,... | collective-permute-start | bytes 98312 | tf_op jit(solution)/shard_map/ppermute | solution.py:20
Sparse Core Ops, SparseCore 0:
  52.1 12.4 reduce-scatter.1
where the time goes:
time: 299 us; the launch traced here: 296 us
  local copies, waits for them, and re-layouts  101 us (34%)
  matrix products  73.3 us (25%)
  waiting for transfers between devices  40.3 us (13%)
  blocking collectives  29.3 us (10%)
  other arithmetic  28.7 us (10%)
  between operations  13.9 us (5%)
  starting transfers between devices  8.78 us (3%)
    unnamed x24, local copies, waits for them, and re-layouts  51.1 us
    all_to_all x1, blocking collectives, encode_return(): lax.all_to_all(encoded, 'tm', split_axis=0, concat_axis=1, tiled=True)  29.3 us
    all_to_all x1, waiting for transfers between devices, body(): lax.all_to_all(sectioned, 'tm', split_axis=1, concat_axis=0, tiled=True)  26 us
    reduce_sum x8, other arithmetic, one_block(): jnp.sum(jnp.where(matches, weights[:, None, :], jnp.zeros_like(weights[:,...  20 us
    dot_general x2, matrix products, encode_stack(): jnp.einsum('fchd,gchd->chfg', projected[:, :, 0], projected[:, :, 1], pre...  18 us
    dot_general x8, matrix products, one_block(): jnp.dot(matrix, features, preferred_element_type=jnp.float32)  15.7 us
    dot_general x2, matrix products, encode_stack(): jnp.einsum('chfg,gchd->fchd', soft_weights, projected[:, :, 2], preferred...  15.5 us
    convert_element_type x2, local copies, waits for them, and re-layouts, encode_stack(): (raised / jnp.sum(raised, axis=-1, keepdims=True)).astype(jnp.bfloat16)  12.8 us
  transfers between devices with their start and end apart: 4, of which 3 were waited for; matrix products, arithmetic and copies ran while one was open for 0% of the time, Pallas kernels for 0%

commit v1 on v0

--- a/solution.py
+++ b/solution.py
@@ -1,10 +1,28 @@
+import functools
 import jax
 import jax.numpy as jnp
 from jax import lax
 from jax.sharding import PartitionSpec as P
+from jax.lax import all_to_all, axis_size
 
 HEADS = 8
 GRID = 64
+
+
+def take_bars(original, lane_axis):
+    piece_now = jnp.concatenate(
+        all_to_all(
+            jnp.stack(jnp.split(original, axis_size(lane_axis), axis=0)),
+            axis_name=lane_axis,
+            split_axis=0,
+            concat_axis=0,
+        ),
+        axis=1,
+    )
+    return piece_now
+
+
+_put_cubes = functools.partial(take_bars, lane_axis="tm")
 
 
 def padded_2(cells, sides, width):
@@ -93,7 +111,7 @@
 
 def encode_return(tokens, weights):
     encoded = encode_stack(tokens, *weights)
-    return lax.all_to_all(encoded, "tm", split_axis=0, concat_axis=1, tiled=True)
+    return _put_cubes(encoded)
 
 
 def body(

time: 299 us -> 313 us (1.047)
  local copies, waits for them, and re-layouts: 101 us -> 113 us
  matrix products: 73.3 us -> 77.3 us
  waiting for transfers between devices: 40.3 us -> 36.6 us
    convert_element_type x0 -> x2, local copies, waits for them, and re-layouts: none -> 3.37 us  [the longest x1 1.74 us: encode_stack(): tokens.astype(jnp.float32) + time_embed[:, None, :].astype(jnp.float32)]
    unnamed x24 -> x43, local copies, waits for them, and re-layouts: 51.1 us -> 53.4 us
  transfers between devices with their start and end apart: 4 -> 4, of which waited for: 3 -> 2; matrix products, arithmetic and copies ran while one was open for 0% -> 2% of each run, Pallas kernels for 0% -> 0%
where the time goes in v1:
time: 313 us; the launch traced here: 308 us
  local copies, waits for them, and re-layouts  113 us (36%)
  matrix products  77.3 us (25%)
  waiting for transfers between devices  36.6 us (12%)
  blocking collectives  29.5 us (9%)
  other arithmetic  27.9 us (9%)
  between operations  14.2 us (5%)
  starting transfers between devices  8.96 us (3%)
    unnamed x43, local copies, waits for them, and re-layouts  53.4 us
    all_to_all x1, blocking collectives, take_bars(): all_to_all(jnp.stack(jnp.split(original, axis_size(lane_axis), axis=0)),...  29.5 us
    all_to_all x1, waiting for transfers between devices, body(): lax.all_to_all(sectioned, 'tm', split_axis=1, concat_axis=0, tiled=True)  23.9 us
    reduce_sum x8, other arithmetic, one_block(): jnp.sum(jnp.where(matches, weights[:, None, :], jnp.zeros_like(weights[:,...  20 us
    dot_general x2, matrix products, encode_stack(): jnp.einsum('fchd,gchd->chfg', projected[:, :, 0], projected[:, :, 1], pre...  18 us
    dot_general x8, matrix products, one_block(): jnp.dot(matrix, features, preferred_element_type=jnp.float32)  15.6 us
    dot_general x2, matrix products, encode_stack(): jnp.einsum('chfg,gchd->fchd', soft_weights, projected[:, :, 2], preferred...  15.5 us
    dot_general x2, matrix products, encode_stack(): jnp.dot(hidden_units, w_down[number], preferred_element_type=jnp.float32)  13.6 us
  transfers between devices with their start and end apart: 4, of which 2 were waited for; matrix products, arithmetic and copies ran while one was open for 2% of the time, Pallas kernels for 0%

profile of v1, /device:TPU:0, one launch (start us, length us, event | category | flops | bytes accessed | tf_op | source)
XLA Modules:
  0.0 308.2 jit_solution(12580949665610882996)
XLA Ops:
  6.5 44.5 %while.17 = (s32[]{:T(128)}, bf16[8,512,256]{2,1,0:T(8,128)(2,1)}, s32[1,16,512]{2,1,0:T(8,128)}, s32[8]{0:T(128)S(1)}, f32[16,512]{1,0:T(8,128)}, /*index=5*/bf16[512,256]{1,0:T(8,128)(2,1)}, s32[]{:T(128)}) while((s32[]{:T(128)}, bf16[8,512,256]{2,1,0:T(8,128)(2,1)}, s32[1,16,512]{2,1,0:T(8,128)}, s32[8]{0:T(128)S(1)}, f32[16,512]{1,0:T(8,128)}, ...), condition=%wide.region_2.3_spmd, body=%wide.region_0.2_spmd.sunk | while | flops 146670080 | bytes 1643101 | solution.py:64
  51.1 12.6 %reduce-scatter.2.cloned.1.call-done = bf16[1,2048,256]{2,1,0:T(8,128)(2,1)} async-done(((bf16[1,4096,256]{2,1,0:T(8,128)(2,1)}), bf16[1,2048,256]{2,1,0:T(8,128)(2,1)}) %reduce-scatter.2.cloned.1.call-update) | async-done | bytes 1048592 | tf_op jit(solution)/shard_map/reduce_scatter | solution.py:127
  66.0 6.4 %all-to-all-start = ((bf16[1,8,256,256]{2,3,0,1:T(8,128)(2,1)}), bf16[1,8,256,256]{2,3,0,1:T(8,128)(2,1)S(1)}, u32[]{:S(2)}, u32[]{:S(2)}) async-start(bf16[1,8,256,256]{2,3,0,1:T(8,128)(2,1)} %copy.94), calls=%async_computation.1 | async-start | bytes 2097152 | tf_op jit(solution)/shard_map/all_to_all | solution.py:132
  74.5 23.9 %all-to-all-done = bf16[1,8,256,256]{2,3,0,1:T(8,128)(2,1)S(1)} async-done(((bf16[1,8,256,256]{2,3,0,1:T(8,128)(2,1)}), bf16[1,8,256,256]{2,3,0,1:T(8,128)(2,1)S(1)}, u32[]{:S(2)}, u32[]{:S(2)}) %all-to-all-start) | async-done | bytes 1048608 | tf_op jit(solution)/shard_map/all_to_all | solution.py:132
  107.6 7.2 %copy.119 = bf16[8,256,1,8,32]{4,0,3,1,2:T(8,128)(2,1)} copy(bf16[8,256,1,8,32]{1,0,4,3,2:T(8,128)(2,1)S(1)} %get-tuple-element.69) | data formatting | bytes 2097152
  114.8 7.2 %copy.120 = bf16[8,256,1,8,32]{4,0,3,1,2:T(8,128)(2,1)} copy(bf16[8,256,1,8,32]{1,0,4,3,2:T(8,128)(2,1)S(1)} %get-tuple-element.70) | data formatting | bytes 2097152
  121.9 9.0 %fusion.26 = f32[256,8,8,8]{2,3,1,0:T(8,128)} fusion(bf16[8,256,1,8,32]{4,0,3,1,2:T(8,128)(2,1)} %copy.120, bf16[8,256,1,8,32]{4,0,3,1,2:T(8,128)(2,1)} %copy.119), kind=kOutput, calls=%fused_computation.31 | convolution fusion | flops 8388608 | bytes 2621440 | tf_op jit(solution)/shard_map/fchd,gchd->chfg/dot_general | solution.py:88
  131.0 6.4 %copy.102 = f32[256,8,8,8]{0,3,2,1:T(8,128)S(1)} copy(f32[256,8,8,8]{2,3,1,0:T(8,128)} %fusion.26) | data formatting | bytes 1048576 | tf_op jit(solution)/shard_map/fchd,gchd->chfg/dot_general | solution.py:88
  138.4 6.4 %copy.103 = bf16[256,8,8,8]{3,2,1,0:T(8,128)(2,1)} copy(bf16[256,8,8,8]{0,3,2,1:T(8,128)(2,1)S(1)} %divide_convert_fusion.1) | data formatting | bytes 524288 | tf_op jit(solution)/shard_map/convert_element_type | solution.py:97
  144.8 7.4 %copy.118 = bf16[8,256,1,8,32]{4,0,3,1,2:T(8,128)(2,1)} copy(bf16[8,256,1,8,32]{1,0,4,3,2:T(8,128)(2,1)S(1)} %get-tuple-element.68) | data formatting | bytes 2097152
  152.2 7.7 %convert_bitcast_fusion.1 = bf16[8,256,8,32]{3,0,2,1:T(8,128)(2,1)} fusion(bf16[256,8,8,8]{3,2,1,0:T(8,128)(2,1)} %copy.103, bf16[8,256,1,8,32]{4,0,3,1,2:T(8,128)(2,1)} %copy.118), kind=kOutput, calls=%fused_computation.37 | convolution fusion | flops 8912896 | bytes 2359296 | tf_op jit(solution)/shard_map/chfg,gchd->fchd/dot_general | solution.py:98
  159.9 6.8 %copy.104 = bf16[8,256,8,32]{1,0,3,2:T(8,128)(2,1)} copy(bf16[8,256,8,32]{3,0,2,1:T(8,128)(2,1)} %convert_bitcast_fusion.1) | data formatting | bytes 2097152 | tf_op jit(solution)/shard_map/convert_element_type | solution.py:100
  171.1 3.8 %multiply_reduce_fusion.2 = (f32[2048]{0:T(1024)S(1)}, f32[2048,256]{0,1:T(8,128)}) fusion(bf16[2048,256]{0,1:T(8,128)(2,1)} %bitcast.196, bf16[2,256,256]{2,1,0:T(8,128)(2,1)S(1)} %copy-done.10, f32[2048,256]{0,1:T(8,128)} %copy.116, f32[2048,256]{0,1:T(8,128)S(1)} %copy-done.2), kind=kOutput, calls=%fused_computation.81 | convolution fusion | flops 270530560 | bytes 7479296 | tf_op jit(solution)/shard_map/dot_general | solution.py:102
  174.9 7.5 %multiply_reduce_fusion.1 = (f32[2048]{0:T(1024)S(1)}, f32[2048,256]{0,1:T(8,128)}) fusion(f32[2048,256]{0,1:T(8,128)} %get-tuple-element.89, bf16[2,1024,256]{2,1,0:T(8,128)(2,1)} %param.20, f32[256]{0:T(256)S(1)} %bitcast.209, f32[2048]{0:T(1024)S(1)} %add_rsqrt_fusion.2, bf16[2,256,1024]{2,1,0:T(8,128)(2,1)} %param.19), kind=kOutput, calls=%fused_computation.79 | convolution fusion | flops 2169501696 | bytes 7357440 | tf_op jit(solution)/shard_map/dot_general | solution.py:108
  191.5 7.2 %copy.122 = bf16[8,256,1,8,32]{4,0,3,1,2:T(8,128)(2,1)} copy(bf16[8,256,1,8,32]{1,0,4,3,2:T(8,128)(2,1)S(1)} %get-tuple-element.66) | data formatting | bytes 2097152
  198.7 7.2 %copy.123 = bf16[8,256,1,8,32]{4,0,3,1,2:T(8,128)(2,1)} copy(bf16[8,256,1,8,32]{1,0,4,3,2:T(8,128)(2,1)S(1)} %get-tuple-element.67) | data formatting | bytes 2097152
  205.9 9.0 %fusion.21 = f32[256,8,8,8]{2,3,1,0:T(8,128)} fusion(bf16[8,256,1,8,32]{4,0,3,1,2:T(8,128)(2,1)} %copy.123, bf16[8,256,1,8,32]{4,0,3,1,2:T(8,128)(2,1)} %copy.122), kind=kOutput, calls=%fused_computation.26 | convolution fusion | flops 8388608 | bytes 2621440 | tf_op jit(solution)/shard_map/fchd,gchd->chfg/dot_general | solution.py:88
  214.9 6.4 %copy.109 = f32[256,8,8,8]{0,3,2,1:T(8,128)S(1)} copy(f32[256,8,8,8]{2,3,1,0:T(8,128)} %fusion.21) | data formatting | bytes 1048576 | tf_op jit(solution)/shard_map/fchd,gchd->chfg/dot_general | solution.py:88
  222.4 6.4 %copy.110 = bf16[256,8,8,8]{3,2,1,0:T(8,128)(2,1)} copy(bf16[256,8,8,8]{0,3,2,1:T(8,128)(2,1)S(1)} %divide_convert_fusion) | data formatting | bytes 524288 | tf_op jit(solution)/shard_map/convert_element_type | solution.py:97
  228.8 7.4 %copy.121 = bf16[8,256,1,8,32]{4,0,3,1,2:T(8,128)(2,1)} copy(bf16[8,256,1,8,32]{1,0,4,3,2:T(8,128)(2,1)S(1)} %get-tuple-element.65) | data formatting | bytes 2097152
  236.2 7.7 %convert_bitcast_fusion = bf16[8,256,8,32]{3,0,2,1:T(8,128)(2,1)} fusion(bf16[256,8,8,8]{3,2,1,0:T(8,128)(2,1)} %copy.110, bf16[8,256,1,8,32]{4,0,3,1,2:T(8,128)(2,1)} %copy.121), kind=kOutput, calls=%fused_computation.36 | convolution fusion | flops 8912896 | bytes 2359296 | tf_op jit(solution)/shard_map/chfg,gchd->fchd/dot_general | solution.py:98
  243.9 6.0 %copy.111 = bf16[8,256,8,32]{1,0,3,2:T(8,128)(2,1)S(1)} copy(bf16[8,256,8,32]{3,0,2,1:T(8,128)(2,1)} %convert_bitcast_fusion) | data formatting | bytes 2097152 | tf_op jit(solution)/shard_map/convert_element_type | solution.py:100
  252.1 6.1 %fusion.70 = bf16[2048,256]{0,1:T(8,128)(2,1)S(1)} fusion(f32[2048,256]{0,1:T(8,128)} %get-tuple-element.95, f32[256]{0:T(256)S(1)} %bitcast.208, f32[2048]{0:T(1024)S(1)} %add_rsqrt_fusion, bf16[2,1024,256]{2,1,0:T(8,128)(2,1)} %param.20, bf16[2,256,1024]{2,1,0:T(8,128)(2,1)} %param.19), kind=kOutput, calls=%fused_computation.72 | convolution fusion | flops 2168979456 | bytes 6300672 | tf_op jit(solution)/shard_map/dot_general | solution.py:108
  258.5 29.5 %all_to_all.14 = bf16[8,1,256,256]{2,3,1,0:T(8,128)(2,1)S(1)} all-to-all(bf16[8,1,256,256]{2,3,1,0:T(8,128)(2,1)S(1)} %fusion.122), channel_id=1, replica_groups=mesh['groups'=2,'tm'=8,'sector'=2] {'tm'}, dimensions={0} | all-to-all | bytes 2097152 | tf_op jit(solution)/shard_map/all_to_all | solution.py:14
  (112 shorter events, 88.6 us)
Async XLA Ops:
  6.5 57.2 %reduce-scatter.2.cloned.1.call-start = ((), (), s32[]{:S(2)}) async-start(), calls=%async_computation.3 | async-start | bytes 3145728 | tf_op jit(solution)/shard_map/reduce_scatter | solution.py:127
  51.1 21.3 %copy-start.11 = (bf16[8,256]{1,0:T(8,128)(2,1)S(1)}, bf16[8,256]{1,0:T(8,128)(2,1)}, u32[]{:S(2)}) copy-start(bf16[8,256]{1,0:T(8,128)(2,1)} %param.15) | copy-start | bytes 12292
  66.0 32.4 %all-to-all-start = ((bf16[1,8,256,256]{2,3,0,1:T(8,128)(2,1)}), bf16[1,8,256,256]{2,3,0,1:T(8,128)(2,1)S(1)}, u32[]{:S(2)}, u32[]{:S(2)}) async-start(bf16[1,8,256,256]{2,3,0,1:T(8,128)(2,1)} %copy.94), calls=%async_computation.1 | async-start | bytes 2097152 | tf_op jit(solution)/shard_map/all_to_all | solution.py:132
  72.4 2.1 copy-start.12
  98.9 1.0 copy-start
  98.9 1.5 copy-start.6
  159.9 9.5 %copy-start.1 = (bf16[1,8,256,256]{3,2,1,0:T(8,128)(2,1)S(1)}, bf16[1,8,256,256]{3,2,1,0:T(8,128)(2,1)}, u32[]{:S(2)}) copy-start(bf16[1,8,256,256]{3,2,1,0:T(8,128)(2,1)} %copy-done) | copy-start | bytes 3145732
  166.7 4.4 %copy-start.2 = (f32[2048,256]{0,1:T(8,128)S(1)}, f32[2048,256]{0,1:T(8,128)}, u32[]{:S(2)}) copy-start(f32[2048,256]{0,1:T(8,128)} %copy.117) | copy-start | bytes 6291460
  166.7 4.4 %copy-start.10 = (bf16[2,256,256]{2,1,0:T(8,128)(2,1)S(1)}, bf16[2,256,256]{2,1,0:T(8,128)(2,1)}, u32[]{:S(2)}) copy-start(bf16[2,256,256]{2,1,0:T(8,128)(2,1)} %param.18) | copy-start | bytes 786436
  243.9 6.3 %copy-start.3 = (f32[2048,256]{0,1:T(8,128)S(1)}, f32[2048,256]{0,1:T(8,128)}, u32[]{:S(2)}) copy-start(f32[2048,256]{0,1:T(8,128)} %get-tuple-element.91) | copy-start | bytes 6291460
  258.3 32.8 %copy-start.5 = (bf16[3,3,256,256]{3,2,1,0:T(8,128)(2,1)S(1)}, bf16[3,3,256,256]{3,2,1,0:T(8,128)(2,1)}, u32[]{:S(2)}) copy-start(bf16[3,3,256,256]{3,2,1,0:T(8,128)(2,1)} %param.21) | copy-start | bytes 3538948
  288.5 5.3 %collective-permute-start = (bf16[1,1,64,256]{3,2,1,0:T(8,128)(2,1)S(1)}, bf16[1,1,64,256]{3,2,1,0:T(8,128)(2,1)S(1)}, u32[]{:S(2)}, u32[]{:S(2)}) collective-permute-start(bf16[1,1,64,256]{3,2,1,0:T(8,128)(2,1)S(1)} %get-tuple-element.80), channel_id=1, source_target_pairs={{0,1},{2,3},{4,5},{6,7},{8,9},{10,11},{12,13},{14,15},{16,17},{18,... | collective-permute-start | bytes 98312 | tf_op jit(solution)/shard_map/ppermute | solution.py:36
  289.8 4.0 %collective-permute-start.1 = (bf16[1,1,64,256]{3,2,1,0:T(8,128)(2,1)S(1)}, bf16[1,1,64,256]{3,2,1,0:T(8,128)(2,1)S(1)}, u32[]{:S(2)}, u32[]{:S(2)}) collective-permute-start(bf16[1,1,64,256]{3,2,1,0:T(8,128)(2,1)S(1)} %get-tuple-element.81), channel_id=1, source_target_pairs={{1,0},{3,2},{5,4},{7,6},{9,8},{11,10},{13,12},{15,14},{17,16},{19,... | collective-permute-start | bytes 98312 | tf_op jit(solution)/shard_map/ppermute | solution.py:38
  294.5 1.1 copy-start.9
  295.6 1.6 copy-start.8
  297.2 1.6 copy-start.4
  297.2 1.6 copy-start.7
Sparse Core Ops, SparseCore 0:
  51.2 12.4 reduce-scatter.1
